TPU v7x, 32 devices: a whole 2x2x4 slice. The times are simulated.
32 devices in a mesh: dp: 8 (over y, x, core), tensor: 4 (over z).
Axes of the slice: x: 2, y: 2, z: 4, core: 2. Of those that a mesh axis runs over, the one named last changes fastest.
Arguments:
- inputs: bfloat16 [12288, 768], P(('dp', 'tensor')), may hold values from -6 to 6
- segments: int32 [24, 512], P('dp'), may hold values from 0 to 3, never falling along the last dimension, each value on 1 to 256 neighbouring positions
- labels: int32 [24], P('dp'), may hold values from 0 to 2
- qkv_weight: bfloat16 [3, 768, 768], P(None, None, 'tensor'), may hold values from -0.21875 to 0.21875
- qv_bias: float32 [2, 768], P(None, 'tensor'), may hold values from -3 to 3
- out_weight: bfloat16 [768, 768], P('tensor'), may hold values from -0.875 to 0.875
- out_bias: float32 [768], replicated, may hold values from -3 to 3
- norm1_gain: float32 [768], replicated, may hold values from 0.5 to 1.5
- norm1_bias: float32 [768], replicated, may hold values from -3 to 3
- up_weight: bfloat16 [768, 3072], P(None, 'tensor'), may hold values from -0.21875 to 0.21875
- up_bias: float32 [3072], P('tensor'), may hold values from -3 to 3
- down_weight: bfloat16 [3072, 768], P('tensor'), may hold values from -0.109375 to 0.109375
- down_bias: float32 [768], replicated, may hold values from -3 to 3
- norm2_gain: float32 [768], replicated, may hold values from 0.5 to 1.5
- norm2_bias: float32 [768], replicated, may hold values from -3 to 3
- pool_weight: bfloat16 [768, 768], replicated, may hold values from -0.21875 to 0.21875
- pool_bias: float32 [768], replicated, may hold values from -3 to 3
- class_weight: bfloat16 [768, 3], replicated, may hold values from -0.4375 to 0.4375
- class_bias: float32 [3], replicated, may hold values from -4 to 4
- cotangent: bfloat16 [12288, 768], P(('dp', 'tensor')), may hold values from -6 to 6
Outputs:
- hidden: bfloat16 [12288, 768], P(('dp', 'tensor'))
- input_grad: bfloat16 [12288, 768], P(('dp', 'tensor'))
- qkv_weight_grad: float32 [3, 768, 768], P(None, 'dp', 'tensor')
- qv_bias_grad: float32 [2, 768], P(None, 'tensor')
- out_weight_grad: float32 [768, 768], P('tensor', 'dp')
- out_bias_grad: float32 [768], replicated
- norm1_gain_grad: float32 [768], replicated
- norm1_bias_grad: float32 [768], replicated
- up_weight_grad: float32 [768, 3072], P('dp', 'tensor')
- up_bias_grad: float32 [3072], P('tensor')
- down_weight_grad: float32 [3072, 768], P('tensor', 'dp')
- down_bias_grad: float32 [768], replicated
- norm2_gain_grad: float32 [768], replicated
- norm2_bias_grad: float32 [768], replicated
- pool_weight_grad: float32 [768, 768], replicated
- pool_bias_grad: float32 [768], replicated
- class_weight_grad: float32 [768, 3], replicated
- class_bias_grad: float32 [3], replicated
Inputs may be any that keep to these rules, and one draw needn't show every extreme that they name: `segments`: along each packed row of 512 tokens the ids never fall; a document holds at most half of 512 tokens.
All inputs are finite; a program needn't handle non-finite values.
Results may differ from a plain program's by a relative error of at most 0.017.
The roundings to bfloat16 on the way count: a program that leaves them out, or rounds other values in their place, can miss the bound.
Values may be sent and summed in bfloat16 or wider, within the bound.
A program may use at most 128 MiB of HBM per device.

v0:
```python
from functools import partial
import jax
import jax.numpy as jnp
from jax import lax
from jax.sharding import PartitionSpec as P

HEAD = 64
epsilon = 1e-12
masked_value = -1e30


def norm_forward(values, norm_gain, norm_shift):
    centre = values - jnp.mean(values, axis=-1, keepdims=True)
    inverse = lax.rsqrt(jnp.mean(centre * centre, axis=-1, keepdims=True) + epsilon)
    normed = centre * inverse
    return (normed * norm_gain + norm_shift, normed, inverse)


def norm_backward(grad_out, normed, inverse, norm_gain):
    scaled = grad_out * norm_gain
    grad_in = inverse * (
        scaled
        - jnp.mean(scaled, axis=-1, keepdims=True)
        - normed * jnp.mean(scaled * normed, axis=-1, keepdims=True)
    )
    return (grad_in, jnp.sum(grad_out * normed, axis=0), jnp.sum(grad_out, axis=0))


def split_heads(rows):
    return rows.reshape(rows.shape[0], rows.shape[1] // HEAD, HEAD)


def masked_scores(query_heads, key_heads, segment_row):
    raw_scores = jnp.einsum(
        "qhe,khe->hqk", query_heads, key_heads, preferred_element_type=jnp.float32
    ) * HEAD ** (-0.5)
    allowed = segment_row[:, None] == segment_row[None, :]
    return (jnp.where(allowed[None], raw_scores, masked_value), allowed)


def attend_sequence(block_items):
    query_seq, key_seq, value_seq, segment_row = block_items
    scores, allowed = masked_scores(split_heads(query_seq), split_heads(key_seq), segment_row)
    largest = jnp.max(scores, axis=-1, keepdims=True)
    exponent = jnp.exp(scores - largest)
    row_total = jnp.sum(exponent, axis=-1, keepdims=True)
    soft_low = (exponent / row_total).astype(jnp.bfloat16)
    context = jnp.einsum(
        "hqk,khe->qhe", soft_low, split_heads(value_seq), preferred_element_type=jnp.float32
    )
    context = context.reshape(query_seq.shape).astype(jnp.bfloat16)
    return (context, largest[..., 0] + jnp.log(row_total[..., 0]))


def attend_backward(block_items):
    query_seq, key_seq, value_seq, segment_row, log_total, grad_context = block_items
    query_heads = split_heads(query_seq)
    key_heads = split_heads(key_seq)
    value_heads = split_heads(value_seq)
    grad_heads = split_heads(grad_context)
    scores, allowed = masked_scores(query_heads, key_heads, segment_row)
    soft_probs = jnp.exp(scores - log_total[..., None])
    grad_values = jnp.einsum(
        "hqk,qhe->khe",
        soft_probs.astype(jnp.bfloat16),
        grad_heads,
        preferred_element_type=jnp.float32,
    )
    grad_soft = jnp.einsum(
        "qhe,khe->hqk", grad_heads, value_heads, preferred_element_type=jnp.float32
    )
    grad_scores = soft_probs * (grad_soft - jnp.sum(soft_probs * grad_soft, axis=-1, keepdims=True))
    grad_low = jnp.where(allowed[None], grad_scores, 0.0).astype(jnp.bfloat16)
    score_scale = HEAD ** (-0.5)
    grad_queries = (
        jnp.einsum("hqk,khe->qhe", grad_low, key_heads, preferred_element_type=jnp.float32)
        * score_scale
    )
    grad_keys = (
        jnp.einsum("hqk,qhe->khe", grad_low, query_heads, preferred_element_type=jnp.float32)
        * score_scale
    )
    full_shape = query_seq.shape
    return (
        grad_queries.reshape(full_shape).astype(jnp.bfloat16),
        grad_keys.reshape(full_shape).astype(jnp.bfloat16),
        grad_values.reshape(full_shape).astype(jnp.bfloat16),
    )


def body(
    inputs,
    segments,
    labels,
    qkv_weight,
    qv_bias,
    out_weight,
    out_bias,
    norm1_gain,
    norm1_bias,
    up_weight,
    up_bias,
    down_weight,
    down_bias,
    norm2_gain,
    norm2_bias,
    pool_weight,
    pool_bias,
    class_weight,
    class_bias,
    cotangent,
):
    share_rows = inputs.shape[0]
    seq_count, seq_length = segments.shape
    offset = lax.axis_index("tensor") * share_rows

    def take_share(array):
        return lax.dynamic_slice_in_dim(array, offset, share_rows, 0)

    gathered = lax.all_gather(inputs, "tensor", axis=0, tiled=True)
    group_rows = gathered.shape[0]
    projected = jnp.einsum("td,kde->kte", gathered, qkv_weight, preferred_element_type=jnp.float32)
    queries = (projected[0] + qv_bias[0]).astype(jnp.bfloat16)
    key_rows = projected[1].astype(jnp.bfloat16)
    value_rows = (projected[2] + qv_bias[1]).astype(jnp.bfloat16)
    local_width = queries.shape[1]

    def by_sequence(rows):
        return rows.reshape(seq_count, seq_length, rows.shape[-1])

    context, log_totals = lax.map(
        attend_sequence,
        (by_sequence(queries), by_sequence(key_rows), by_sequence(value_rows), segments),
    )
    context = context.reshape(group_rows, local_width)
    attended_all = (
        lax.psum(jnp.dot(context, out_weight, preferred_element_type=jnp.float32), "tensor")
        + out_bias
    )
    first_whole, normed_whole, inverse_whole = norm_forward(
        gathered.astype(jnp.float32) + attended_all, norm1_gain, norm1_bias
    )
    first_all = first_whole.astype(jnp.bfloat16)
    normed_one = take_share(normed_whole)
    inverse_one = take_share(inverse_whole)
    up_pre = jnp.dot(first_all, up_weight, preferred_element_type=jnp.float32) + up_bias
    gelu_exact = partial(jax.nn.gelu, approximate=False)
    active = gelu_exact(up_pre).astype(jnp.bfloat16)
    ffn_all = (
        lax.psum(jnp.dot(active, down_weight, preferred_element_type=jnp.float32), "tensor")
        + down_bias
    )
    final_whole, normed_all, inverse_all = norm_forward(
        first_whole + ffn_all, norm2_gain, norm2_bias
    )
    final_norm = take_share(final_whole)
    normed_two = take_share(normed_all)
    inverse_two = take_share(inverse_all)
    positions = offset + jnp.arange(share_rows, dtype=jnp.int32)
    row_starts = jnp.arange(seq_count, dtype=jnp.int32) * seq_length
    selector = (row_starts[:, None] == positions[None, :]).astype(jnp.float32)
    leading_part = jnp.dot(selector, final_norm, precision=lax.Precision.HIGHEST)
    leading = lax.psum(leading_part, "tensor").astype(jnp.bfloat16)
    pooled = jnp.tanh(jnp.dot(leading, pool_weight, preferred_element_type=jnp.float32) + pool_bias)
    pooled_low = pooled.astype(jnp.bfloat16)
    logits = jnp.dot(pooled_low, class_weight, preferred_element_type=jnp.float32) + class_bias
    chosen = (
        labels[:, None] == jnp.arange(class_weight.shape[1], dtype=jnp.int32)[None, :]
    ).astype(jnp.float32)
    grad_logits = (jax.nn.softmax(logits, axis=-1) - chosen).astype(jnp.bfloat16)
    class_weight_grad = jnp.einsum(
        "rd,rc->dc", pooled_low, grad_logits, preferred_element_type=jnp.float32
    )
    class_bias_grad = jnp.sum(grad_logits.astype(jnp.float32), axis=0)
    grad_pre = (
        jnp.einsum("rc,dc->rd", grad_logits, class_weight, preferred_element_type=jnp.float32)
        * (1.0 - pooled * pooled)
    ).astype(jnp.bfloat16)
    pool_weight_grad = jnp.einsum(
        "rd,re->de", leading, grad_pre, preferred_element_type=jnp.float32
    )
    pool_bias_grad = jnp.sum(grad_pre.astype(jnp.float32), axis=0)
    grad_leading = jnp.einsum(
        "re,de->rd", grad_pre, pool_weight, preferred_element_type=jnp.float32
    )
    grad_final = cotangent.astype(jnp.float32) + jnp.einsum(
        "rt,rd->td", selector, grad_leading, precision=lax.Precision.HIGHEST
    )
    grad_second, norm2_gain_grad, norm2_bias_grad = norm_backward(
        grad_final, normed_two, inverse_two, norm2_gain
    )
    grad_fed = grad_second.astype(jnp.bfloat16)
    down_bias_grad = jnp.sum(grad_fed.astype(jnp.float32), axis=0)
    grad_fed_all = lax.all_gather(grad_fed, "tensor", axis=0, tiled=True)
    down_weight_grad = jnp.einsum(
        "tf,td->fd", active, grad_fed_all, preferred_element_type=jnp.float32
    )
    grad_active = jnp.einsum(
        "td,fd->tf", grad_fed_all, down_weight, preferred_element_type=jnp.float32
    )
    grad_up = jax.vjp(gelu_exact, up_pre)[1](grad_active)[0].astype(jnp.bfloat16)
    up_bias_grad = jnp.sum(grad_up.astype(jnp.float32), axis=0)
    up_weight_grad = jnp.einsum("td,tf->df", first_all, grad_up, preferred_element_type=jnp.float32)
    grad_first = (
        lax.psum_scatter(
            jnp.einsum("tf,df->td", grad_up, up_weight, preferred_element_type=jnp.float32),
            "tensor",
            scatter_dimension=0,
            tiled=True,
        )
        + grad_second
    )
    grad_res, norm1_gain_grad, norm1_bias_grad = norm_backward(
        grad_first, normed_one, inverse_one, norm1_gain
    )
    grad_att = grad_res.astype(jnp.bfloat16)
    out_bias_grad = jnp.sum(grad_att.astype(jnp.float32), axis=0)
    grad_att_all = lax.all_gather(grad_att, "tensor", axis=0, tiled=True)
    out_weight_grad = jnp.einsum(
        "te,td->ed", context, grad_att_all, preferred_element_type=jnp.float32
    )
    grad_context = jnp.einsum(
        "td,ed->te", grad_att_all, out_weight, preferred_element_type=jnp.float32
    ).astype(jnp.bfloat16)
    grad_queries, grad_keys, grad_values = lax.map(
        attend_backward,
        (
            by_sequence(queries),
            by_sequence(key_rows),
            by_sequence(value_rows),
            segments,
            log_totals,
            by_sequence(grad_context),
        ),
    )
    stacked = jnp.stack(
        [
            grad_queries.reshape(group_rows, local_width),
            grad_keys.reshape(group_rows, local_width),
            grad_values.reshape(group_rows, local_width),
        ]
    )
    qkv_weight_grad = jnp.einsum(
        "td,kte->kde", gathered, stacked, preferred_element_type=jnp.float32
    )
    qv_bias_grad = jnp.stack(
        [
            jnp.sum(stacked[0].astype(jnp.float32), axis=0),
            jnp.sum(stacked[2].astype(jnp.float32), axis=0),
        ]
    )
    input_grad = (
        lax.psum_scatter(
            jnp.einsum(
                "kte,kde->td", stacked, qkv_weight, preferred_element_type=jnp.float32
            ).astype(jnp.bfloat16),
            "tensor",
            scatter_dimension=0,
            tiled=True,
        ).astype(jnp.float32)
        + grad_res
    ).astype(jnp.bfloat16)
    qkv_sum, out_sum, up_sum, down_sum = (
        lax.psum_scatter(qkv_weight_grad, "dp", scatter_dimension=1, tiled=True),
        lax.psum_scatter(out_weight_grad, "dp", scatter_dimension=1, tiled=True),
        lax.psum_scatter(up_weight_grad, "dp", scatter_dimension=0, tiled=True),
        lax.psum_scatter(down_weight_grad, "dp", scatter_dimension=1, tiled=True),
    )
    token_grads = lax.psum(
        (
            out_bias_grad,
            norm1_gain_grad,
            norm1_bias_grad,
            down_bias_grad,
            norm2_gain_grad,
            norm2_bias_grad,
        ),
        ("dp", "tensor"),
    )
    group_grads = lax.psum(
        (
            qv_bias_grad,
            up_bias_grad,
            pool_weight_grad,
            pool_bias_grad,
            class_weight_grad,
            class_bias_grad,
        ),
        "dp",
    )
    return (
        final_norm.astype(jnp.bfloat16),
        input_grad,
        qkv_sum,
        group_grads[0],
        out_sum,
        token_grads[0],
        token_grads[1],
        token_grads[2],
        up_sum,
        group_grads[1],
        down_sum,
        token_grads[3],
        token_grads[4],
        token_grads[5],
        group_grads[2],
        group_grads[3],
        group_grads[4],
        group_grads[5],
    )


def solution(mesh):
    placed = (
        P(("dp", "tensor"), None),
        P("dp", None),
        P("dp"),
        P(None, None, "tensor"),
        P(None, "tensor"),
        P("tensor", None),
        P(),
        P(),
        P(),
        P(None, "tensor"),
        P("tensor"),
        P("tensor", None),
        P(),
        P(),
        P(),
        P(),
        P(),
        P(),
        P(),
        P(("dp", "tensor"), None),
    )
    return jax.shard_map(
        body,
        mesh=mesh,
        in_specs=placed,
        out_specs=(
            P(("dp", "tensor"), None),
            P(("dp", "tensor"), None),
            P(None, "dp", "tensor"),
            P(None, "tensor"),
            P("tensor", "dp"),
            P(),
            P(),
            P(),
            P("dp", "tensor"),
            P("tensor"),
            P("tensor", "dp"),
            P(),
            P(),
            P(),
            P(),
            P(),
            P(),
            P(),
        ),
        check_vma=False,
    )
```

profile of v0, /device:TPU:0, one launch (start us, length us, event | category | flops | bytes accessed | tf_op | source)
XLA Modules:
  0.0 1093.7 jit_solution(14431650405853245202)
XLA Ops:
  8.8 53.6 %all-gather.4.cloned.1.call-done = bf16[1536,768]{1,0:T(8,128)(2,1)} async-done(((bf16[384,768]{1,0:T(8,128)(2,1)}), bf16[1536,768]{1,0:T(8,128)(2,1)}) %all-gather.4.cloned.1.call-update) | async-done | bytes 2359312 | tf_op jit(solution)/shard_map/all_gather | solution.py:120
  76.6 12.6 %while.26 = (s32[]{:T(128)}, bf16[3,512,192]{1,2,0:T(8,128)(2,1)S(1)}, f32[3,3,512]{2,1,0:T(4,128)}, bf16[3,512,192]{1,2,0:T(8,128)(2,1)S(1)}, s32[3,512]{1,0:T(...) while((s32[]{:T(128)}, bf16[3,512,192]{1,2,0:T(8,128)(2,1)S(1)}, ...), condition=%wide.region_3.4_spmd, body=%wide.region_0.3_spmd.sunk | while | flops 211122688 | bytes 12902513 | solution.py:131
  94.9 170.5 %all-reduce.6.cloned.1.call-done = f32[1536,768]{1,0:T(8,128)} async-done(((f32[1536,768]{1,0:T(8,128)}), f32[1536,768]{1,0:T(8,128)}) %all-reduce.6.cloned.1.call-update) | async-done | bytes 4718608 | tf_op jit(solution)/shard_map/psum | solution.py:137
  272.2 13.3 %multiply_convert_fusion = (bf16[1536,768]{1,0:T(8,128)(2,1)S(1)}, f32[1536,768]{1,0:T(8,128)}, f32[1536,768]{1,0:T(8,128)}) fusion(f32[768]{0:T(1024)S(1)} %copy-done.40, bf16[768,768]{1,0:T(8,128)(2,1)S(1)} %copy-done, f32[1536,768]{1,0:T(8,128)S(1)} %subtract_multiply_fusion.1, f32[768]{0:T(1024)S(1)} %copy-done.35, f32[768]{0:T(1024)S(1)} %copy-done.22), kind=kOutput, calls=%fused_computation.53 | convolution fusion | flops 1893335040 | bytes 17703936 | tf_op jit(solution)/shard_map/dot_general | solution.py:146
  286.9 4.2 fusion.93
  291.2 171.0 %all-reduce.8.cloned.1.call-done = f32[1536,768]{1,0:T(8,128)} async-done(((f32[1536,768]{1,0:T(8,128)}), f32[1536,768]{1,0:T(8,128)}) %all-reduce.8.cloned.1.call-update) | async-done | bytes 4718608 | tf_op jit(solution)/shard_map/psum | solution.py:150
  462.2 4.7 fusion.86
  470.8 16.4 %psum.107 = bf16[3,768]{1,0:T(4,128)(2,1)S(1)} all-reduce(f32[3,768]{1,0:T(4,128)S(1)} %fusion.56), channel_id=1, replica_groups=mesh['dp'=8,'tensor'=4] {'tensor'}, use_global_device_ids=true, to_apply=%region_10.11 | all-reduce | flops 2304 | bytes 13824 | tf_op jit(solution)/shard_map/psum | solution.py:163
  496.2 47.9 %all-gather.6.cloned.1.call-done = bf16[1536,768]{1,0:T(8,128)(2,1)} async-done(((bf16[384,768]{1,0:T(8,128)(2,1)}), bf16[1536,768]{1,0:T(8,128)(2,1)}) %all-gather.6.cloned.1.call-update) | async-done | bytes 2359312 | tf_op jit(solution)/shard_map/all_gather | solution.py:194
  544.1 8.8 convert_reduce_fusion
  554.3 4.3 fusion.95
  559.5 83.4 %reduce-scatter.11.cloned.1.call-done = f32[384,768]{1,0:T(8,128)} async-done(((f32[1536,768]{1,0:T(8,128)}), f32[384,768]{1,0:T(8,128)}) %reduce-scatter.11.cloned.1.call-update) | async-done | bytes 1179664 | tf_op jit(solution)/shard_map/reduce_scatter | solution.py:205
  651.2 50.4 %all-gather.8.cloned.1.call-done = bf16[1536,768]{1,0:T(8,128)(2,1)} async-done(((bf16[384,768]{1,0:T(8,128)(2,1)}), bf16[1536,768]{1,0:T(8,128)(2,1)}) %all-gather.8.cloned.1.call-update) | async-done | bytes 2359312 | tf_op jit(solution)/shard_map/all_gather | solution.py:218
  706.1 75.7 %while.27 = (s32[]{:T(128)}, bf16[3,512,192]{1,2,0:T(8,128)(2,1)S(1)}, bf16[3,512,192]{1,2,0:T(8,128)(2,1)}, bf16[3,512,192]{1,2,0:T(8,128)(2,1)S(1)}, bf16[3,51...) while((s32[]{:T(128)}, ...), condition=%wide.region_20.21_spmd, body=%wide.region_18.20_spmd.sunk | while | flops 515084288 | bytes 27811988 | solution.py:225
  716.5 5.8 fusion.176
  724.8 5.8 fusion.178
  741.7 5.8 fusion.176
  750.0 5.8 fusion.178
  767.0 5.8 fusion.176
  775.3 5.8 fusion.178
  801.4 4.3 fusion.49
  805.7 4.2 copy.87
  809.9 4.8 reshape.315
  815.0 4.6 bitcast_convert_fusion
  821.7 6.6 fusion.58
  828.5 5.9 fusion.96
  836.0 40.0 %all-reduce = (f32[768]{0:T(1024)}, f32[768]{0:T(1024)}, f32[768]{0:T(1024)}, f32[768]{0:T(1024)}, f32[768]{0:T(1024)}, /*index=5*/f32[768]{0:T(1024)}) all-reduce(f32[768]{0:T(1024)} %get-tuple-element.275, f32[768]{0:T(1024)} %get-tuple-element.222, ...), channel_id=1, replica_groups=mesh['dp'=8,'tensor'=4] {'dp','tensor'}, use_global_device_ids=true, to_apply=%region_28.29 | all-reduce | flops 4608 | bytes 36864 | tf_op jit(solution)/shard_map/psum | solution.py:269
  876.3 25.2 %all-reduce.1 = (f32[2,192]{1,0:T(2,128)}, f32[768]{0:T(1024)}, f32[768]{0:T(1024)}, f32[768,3]{0,1:T(4,128)}, f32[3]{0:T(128)}) all-reduce(f32[2,192]{1,0:T(2,128)S(1)} %pad_maximum_fusion, f32[768]{0:T(1024)} %get-tuple-element.279, f32[768]{0:T(1024)} %get-tuple-element.301, ...), channel_id=1, replica_groups=mesh['dp'=8,'tensor'=4] {'dp'}, use_global_device_ids=true, to_apply=%region_25.26 | all-reduce | flops 4227 | bytes 33816 | tf_op jit(solution)/shard_map/psum | solution.py:280
  905.0 21.0 %reduce-scatter.13.cloned.1.call-done = bf16[384,768]{1,0:T(8,128)(2,1)} async-done(((bf16[1536,768]{1,0:T(8,128)(2,1)}), bf16[384,768]{1,0:T(8,128)(2,1)}) %reduce-scatter.13.cloned.1.call-update) | async-done | bytes 589840 | tf_op jit(solution)/shard_map/reduce_scatter | solution.py:253
  928.7 62.9 %all-reduce.10.cloned.1.call-done = f32[768,768]{1,0:T(8,128)} async-done(((f32[768,768]{1,0:T(8,128)}), f32[768,768]{1,0:T(8,128)}) %all-reduce.10.cloned.1.call-update) | async-done | bytes 2359312 | tf_op jit(solution)/shard_map/psum | solution.py:280
  991.6 45.7 %reduce-scatter.15.cloned.1.call-done = f32[96,768]{1,0:T(8,128)} async-done(((f32[768,768]{1,0:T(8,128)}), f32[96,768]{1,0:T(8,128)}) %reduce-scatter.15.cloned.1.call-update) | async-done | bytes 294928 | tf_op jit(solution)/shard_map/reduce_scatter | solution.py:266
  1037.2 46.2 %reduce-scatter.17.cloned.1.call-done = f32[768,96]{0,1:T(8,128)} async-done(((f32[768,768]{0,1:T(8,128)}), f32[768,96]{0,1:T(8,128)}) %reduce-scatter.17.cloned.1.call-update) | async-done | bytes 294928 | tf_op jit(solution)/shard_map/reduce_scatter | solution.py:267
  (247 shorter events, 143.9 us)
Async XLA Ops:
  7.2 265.0 %copy-start = (bf16[768,768]{1,0:T(8,128)(2,1)S(1)}, bf16[768,768]{1,0:T(8,128)(2,1)}, u32[]{:S(2)}) copy-start(bf16[768,768]{1,0:T(8,128)(2,1)} %param.33) | copy-start | bytes 3538948
  7.2 55.1 %all-gather.4.cloned.1.call-start = ((), (), s32[]{:S(2)}) async-start(), calls=%async_computation.6 | async-start | bytes 2949120 | tf_op jit(solution)/shard_map/all_gather | solution.py:120
  7.9 257.5 %all-reduce.6.cloned.1.call-start = ((), (), s32[]{:S(2)}) async-start(), calls=%async_computation.7 | async-start | bytes 9437184 | tf_op jit(solution)/shard_map/psum | solution.py:137
  94.5 170.9 %copy-start.3 = (bf16[1536,768]{1,0:T(8,128)(2,1)S(1)}, bf16[1536,768]{1,0:T(8,128)(2,1)}, u32[]{:S(2)}) copy-start(bf16[1536,768]{1,0:T(8,128)(2,1)} %all-gather.4.cloned.1.call-done) | copy-start | bytes 7077892
  94.5 170.9 %copy-start.26 = (f32[768]{0:T(1024)S(1)}, f32[768]{0:T(1024)}, u32[]{:S(2)}) copy-start(f32[768]{0:T(1024)} %param.30) | copy-start | bytes 9220
  94.5 367.7 %all-reduce.8.cloned.1.call-start = ((), (), s32[]{:S(2)}) async-start(), calls=%async_computation.8 | async-start | bytes 9437184 | tf_op jit(solution)/shard_map/psum | solution.py:150
  272.2 13.3 %copy-start.2 = (f32[1536,768]{1,0:T(8,128)}, f32[1536,768]{1,0:T(8,128)S(1)}, u32[]{:S(2)}) copy-start(f32[1536,768]{1,0:T(8,128)S(1)} %subtract_multiply_fusion.1) | copy-start | bytes 14155780
  272.2 14.7 %copy-start.38 = (bf16[768,768]{1,0:T(8,128)(2,1)S(1)}, bf16[768,768]{1,0:T(8,128)(2,1)}, u32[]{:S(2)}) copy-start(bf16[768,768]{1,0:T(8,128)(2,1)} %param.35) | copy-start | bytes 3538948
  291.1 171.1 %copy-start.33 = (f32[768]{0:T(1024)S(1)}, f32[768]{0:T(1024)}, u32[]{:S(2)}) copy-start(f32[768]{0:T(1024)} %param.36) | copy-start | bytes 9220
  291.1 253.0 %all-gather.6.cloned.1.call-start = ((), (), s32[]{:S(2)}) async-start(), calls=%async_computation.9 | async-start | bytes 2949120 | tf_op jit(solution)/shard_map/all_gather | solution.py:194
  467.6 19.7 %copy-start.16 = (bf16[768,768]{1,0:T(8,128)(2,1)S(1)}, bf16[768,768]{1,0:T(8,128)(2,1)}, u32[]{:S(2)}) copy-start(bf16[768,768]{1,0:T(8,128)(2,1)} %param.39) | copy-start | bytes 3538948
  467.6 19.7 %copy-start.34 = (f32[768]{0:T(1024)S(1)}, f32[768]{0:T(1024)}, u32[]{:S(2)}) copy-start(f32[768]{0:T(1024)} %param.40) | copy-start | bytes 9220
  467.6 19.9 %copy-start.39 = (bf16[768,3]{0,1:T(4,128)(2,1)S(1)}, bf16[768,3]{0,1:T(4,128)(2,1)}, u32[]{:S(2)}) copy-start(bf16[768,3]{0,1:T(4,128)(2,1)} %param.41) | copy-start | bytes 13828
  467.6 19.9 %copy-start.42 = (f32[3]{0:T(128)S(1)}, f32[3]{0:T(128)}, u32[]{:S(2)}) copy-start(f32[3]{0:T(128)} %param.42) | copy-start | bytes 40
  467.6 20.1 %copy-start.37 = (s32[3]{0:T(128)S(1)}, s32[3]{0:T(128)}, u32[]{:S(2)}) copy-start(s32[3]{0:T(128)} %param.26) | copy-start | bytes 40
  468.1 21.4 %copy-start.18 = (bf16[384,768]{1,0:T(8,128)(2,1)S(1)}, bf16[384,768]{1,0:T(8,128)(2,1)}, u32[]{:S(2)}) copy-start(bf16[384,768]{1,0:T(8,128)(2,1)} %param.43) | copy-start | bytes 1769476
  489.6 54.5 %copy-start.41 = (f32[768]{0:T(1024)S(1)}, f32[768]{0:T(1024)}, u32[]{:S(2)}) copy-start(f32[768]{0:T(1024)} %param.34) | copy-start | bytes 9220
  495.6 147.2 %reduce-scatter.11.cloned.1.call-start = ((), (), s32[]{:S(2)}) async-start(), calls=%async_computation.10 | async-start | bytes 5898240 | tf_op jit(solution)/shard_map/reduce_scatter | solution.py:205
  558.6 143.0 %all-gather.8.cloned.1.call-start = ((), (), s32[]{:S(2)}) async-start(), calls=%async_computation.11 | async-start | bytes 2949120 | tf_op jit(solution)/shard_map/all_gather | solution.py:218
  559.4 87.5 %copy-start.29 = (f32[384]{0:T(512)}, f32[384]{0:T(512)S(1)}, u32[]{:S(2)}) copy-start(f32[384]{0:T(512)S(1)} %dynamic-slice.6) | copy-start | bytes 4612
  646.9 54.7 %copy-start.19 = (bf16[192,768]{1,0:T(8,128)(2,1)S(1)}, bf16[192,768]{1,0:T(8,128)(2,1)}, u32[]{:S(2)}) copy-start(bf16[192,768]{1,0:T(8,128)(2,1)} %param.29) | copy-start | bytes 884740
  647.0 57.3 %copy-start.30 = (f32[384]{0:T(512)}, f32[384]{0:T(512)S(1)}, u32[]{:S(2)}) copy-start(f32[384]{0:T(512)S(1)} %broadcast_multiply_fusion.2) | copy-start | bytes 4612
  647.0 57.3 %copy-start.31 = (f32[384]{0:T(512)}, f32[384]{0:T(512)S(1)}, u32[]{:S(2)}) copy-start(f32[384]{0:T(512)S(1)} %broadcast_multiply_fusion.3) | copy-start | bytes 4612
  651.0 250.5 %reduce-scatter.21.cloned.1.call-start = ((), (), s32[]{:S(2)}) async-start(), calls=%async_computation.17 | async-start | bytes 884736
  797.5 105.6 %reduce-scatter.19.cloned.1.call-start = ((), (), s32[]{:S(2)}) async-start(), calls=%async_computation.16 | async-start | bytes 2211840
  814.7 111.3 %reduce-scatter.13.cloned.1.call-start = ((), (), s32[]{:S(2)}) async-start(), calls=%async_computation.12 | async-start | bytes 2949120 | tf_op jit(solution)/shard_map/reduce_scatter | solution.py:253
  819.6 171.9 %all-reduce.10.cloned.1.call-start = ((), (), s32[]{:S(2)}) async-start(), calls=%async_computation.15 | async-start | bytes 4718592 | tf_op jit(solution)/shard_map/psum | solution.py:280
  821.7 215.5 %reduce-scatter.15.cloned.1.call-start = ((), (), s32[]{:S(2)}) async-start(), calls=%async_computation.13 | async-start | bytes 2654208 | tf_op jit(solution)/shard_map/reduce_scatter | solution.py:266
  828.4 47.6 %copy-start.14 = (bf16[3,512,192]{1,2,0:T(8,128)(2,1)S(1)}, bf16[3,512,192]{1,2,0:T(8,128)(2,1)}, u32[]{:S(2)}) copy-start(bf16[3,512,192]{1,2,0:T(8,128)(2,1)} %copy-done.13) | copy-start | bytes 1769476
  828.4 254.9 %reduce-scatter.17.cloned.1.call-start = ((), (), s32[]{:S(2)}) async-start(), calls=%async_computation.14 | async-start | bytes 2654208 | tf_op jit(solution)/shard_map/reduce_scatter | solution.py:267
  834.4 41.7 %copy-start.12 = (bf16[3,512,192]{1,2,0:T(8,128)(2,1)S(1)}, bf16[3,512,192]{1,2,0:T(8,128)(2,1)}, u32[]{:S(2)}) copy-start(bf16[3,512,192]{1,2,0:T(8,128)(2,1)} %copy-done.11) | copy-start | bytes 1769476
  834.4 91.7 %copy-start.10 = (f32[384,768]{1,0:T(8,128)S(1)}, f32[384,768]{1,0:T(8,128)}, u32[]{:S(2)}) copy-start(f32[384,768]{1,0:T(8,128)} %copy-done.9) | copy-start | bytes 3538948
  (25 other events, 82.0 us)
Sparse Core Ops, SparseCore 0:
  9.6 52.6 all-gather.3
  94.7 170.7 all-reduce.5
  291.2 170.9 all-reduce.7
  495.7 48.3 all-gather.5
  558.7 84.0 reduce-scatter.10
  651.1 50.4 all-gather.7
  797.7 33.6 reduce-scatter.20
  834.8 40.5 reduce-scatter.18
  878.3 47.6 reduce-scatter.12
  929.2 62.3 all-reduce.9
  995.5 41.6 reduce-scatter.14
  1041.0 42.3 reduce-scatter.16
where the time goes:
time: 1100 us; the launch traced here: 1090 us
  waiting for transfers between devices  753 us (68%)
  matrix products  137 us (12%)
  blocking collectives  81.6 us (7%)
  local copies, waits for them, and re-layouts  73.4 us (7%)
  other arithmetic  31 us (3%)
  between operations  15 us (1%)
    psum x1, waiting for transfers between devices, body(): lax.psum(jnp.dot(active, down_weight, preferred_element_type=jnp.float32)...  171 us
    psum x1, waiting for transfers between devices, body(): lax.psum(jnp.dot(context, out_weight, preferred_element_type=jnp.float32)...  171 us
    reduce_scatter x1, waiting for transfers between devices, body(): lax.psum_scatter(jnp.einsum('tf,df->td', grad_up, up_weight, preferred_el...  83.4 us
    psum x1, waiting for transfers between devices, body(): lax.psum((qv_bias_grad, up_bias_grad, pool_weight_grad, pool_bias_grad, c...  62.9 us
    all_gather x1, waiting for transfers between devices, body(): gathered = lax.all_gather(inputs, 'tensor', axis=0, tiled=True)  53.6 us
    all_gather x1, waiting for transfers between devices, body(): grad_att_all = lax.all_gather(grad_att, 'tensor', axis=0, tiled=True)  50.4 us
    all_gather x1, waiting for transfers between devices, body(): grad_fed_all = lax.all_gather(grad_fed, 'tensor', axis=0, tiled=True)  47.9 us
    reduce_scatter x1, waiting for transfers between devices, body(): lax.psum_scatter(down_weight_grad, 'dp', scatter_dimension=1, tiled=True)  46.2 us
  transfers between devices with their start and end apart: 12, of which 10 were waited for; matrix products, arithmetic and copies ran while one was open for 4% of the time, Pallas kernels for 0%

commit v1 on v0

--- a/solution.py
+++ b/solution.py
@@ -146,9 +146,9 @@
     up_pre = jnp.dot(first_all, up_weight, preferred_element_type=jnp.float32) + up_bias
     gelu_exact = partial(jax.nn.gelu, approximate=False)
     active = gelu_exact(up_pre).astype(jnp.bfloat16)
+    change_bands = lambda original: jnp.sum(lax.all_gather(original, "tensor"), axis=0)
     ffn_all = (
-        lax.psum(jnp.dot(active, down_weight, preferred_element_type=jnp.float32), "tensor")
-        + down_bias
+        change_bands(jnp.dot(active, down_weight, preferred_element_type=jnp.float32)) + down_bias
     )
     final_whole, normed_all, inverse_all = norm_forward(
         first_whole + ffn_all, norm2_gain, norm2_bias

time: 1100 us -> 1260 us (1.15)
  waiting for transfers between devices: 753 us -> 904 us
    all_gather x0 -> x1, waiting for transfers between devices: none -> 322 us  [body(): lax.all_gather(original, 'tensor')]
    psum x1 -> x0, waiting for transfers between devices: 171 us -> none  [body(): lax.psum(jnp.dot(active, down_weight, preferred_element_type=jnp.float32)...]
where the time goes in v1:
time: 1260 us; the launch traced here: 1250 us
  waiting for transfers between devices  904 us (72%)
  matrix products  136 us (11%)
  blocking collectives  81.9 us (7%)
  local copies, waits for them, and re-layouts  73.5 us (6%)
  other arithmetic  41.4 us (3%)
  between operations  15 us (1%)
    all_gather x1, waiting for transfers between devices, body(): lax.all_gather(original, 'tensor')  322 us
    psum x1, waiting for transfers between devices, body(): lax.psum(jnp.dot(context, out_weight, preferred_element_type=jnp.float32)...  171 us
    reduce_scatter x1, waiting for transfers between devices, body(): lax.psum_scatter(jnp.einsum('tf,df->td', grad_up, up_weight, preferred_el...  83.4 us
    psum x1, waiting for transfers between devices, body(): lax.psum((qv_bias_grad, up_bias_grad, pool_weight_grad, pool_bias_grad, c...  62.9 us
    all_gather x1, waiting for transfers between devices, body(): gathered = lax.all_gather(inputs, 'tensor', axis=0, tiled=True)  53.6 us
    all_gather x1, waiting for transfers between devices, body(): grad_att_all = lax.all_gather(grad_att, 'tensor', axis=0, tiled=True)  50.2 us
    all_gather x1, waiting for transfers between devices, body(): grad_fed_all = lax.all_gather(grad_fed, 'tensor', axis=0, tiled=True)  48.4 us
    reduce_scatter x1, waiting for transfers between devices, body(): lax.psum_scatter(up_weight_grad, 'dp', scatter_dimension=0, tiled=True)  46.2 us
  transfers between devices with their start and end apart: 12, of which 10 were waited for; matrix products, arithmetic and copies ran while one was open for 4% of the time, Pallas kernels for 0%

profile of v1, /device:TPU:0, one launch (start us, length us, event | category | flops | bytes accessed | tf_op | source)
XLA Modules:
  0.0 1254.1 jit_solution(7867066773307021685)
XLA Ops:
  8.8 53.6 %all-gather.6.cloned.1.call-done = bf16[1536,768]{1,0:T(8,128)(2,1)} async-done(((bf16[384,768]{1,0:T(8,128)(2,1)}), bf16[1536,768]{1,0:T(8,128)(2,1)}) %all-gather.6.cloned.1.call-update) | async-done | bytes 2359312 | tf_op jit(solution)/shard_map/all_gather | solution.py:120
  76.6 12.6 %while.26 = (s32[]{:T(128)}, bf16[3,512,192]{1,2,0:T(8,128)(2,1)S(1)}, f32[3,3,512]{2,1,0:T(4,128)}, bf16[3,512,192]{1,2,0:T(8,128)(2,1)S(1)}, s32[3,512]{1,0:T(...) while((s32[]{:T(128)}, bf16[3,512,192]{1,2,0:T(8,128)(2,1)S(1)}, ...), condition=%wide.region_3.4_spmd, body=%wide.region_0.3_spmd.sunk | while | flops 211122688 | bytes 12903013 | solution.py:131
  94.8 170.7 %all-reduce.5.cloned.1.call-done = f32[1536,768]{1,0:T(8,128)} async-done(((f32[1536,768]{1,0:T(8,128)}), f32[1536,768]{1,0:T(8,128)}) %all-reduce.5.cloned.1.call-update) | async-done | bytes 4718608 | tf_op jit(solution)/shard_map/psum | solution.py:137
  272.2 13.2 %multiply_convert_fusion = (bf16[1536,768]{1,0:T(8,128)(2,1)S(1)}, f32[1536,768]{1,0:T(8,128)}, f32[1536,768]{1,0:T(8,128)}) fusion(f32[768]{0:T(1024)S(1)} %copy-done.41, bf16[768,768]{1,0:T(8,128)(2,1)S(1)} %copy-done, f32[1536,768]{1,0:T(8,128)S(1)} %subtract_multiply_fusion.1, f32[768]{0:T(1024)S(1)} %copy-done.35, f32[768]{0:T(1024)S(1)} %copy-done.22), kind=kOutput, calls=%fused_computation.53 | convolution fusion | flops 1893335040 | bytes 17703936 | tf_op jit(solution)/shard_map/dot_general | solution.py:146
  286.9 4.2 fusion.93
  291.2 321.6 %all-gather.12.cloned.1.call-done = f32[6144,768]{1,0:T(8,128)} async-done(((f32[1536,768]{1,0:T(8,128)}), f32[6144,768]{1,0:T(8,128)}) %all-gather.12.cloned.1.call-update) | async-done | bytes 18874384 | tf_op jit(solution)/shard_map/all_gather | solution.py:149
  612.8 10.4 reduce_sum.209
  623.3 4.7 fusion.86
  631.9 16.6 %psum.99 = bf16[3,768]{1,0:T(4,128)(2,1)S(1)} all-reduce(f32[3,768]{1,0:T(4,128)S(1)} %fusion.56), channel_id=1, replica_groups=mesh['dp'=8,'tensor'=4] {'tensor'}, use_global_device_ids=true, to_apply=%region_10.11 | all-reduce | flops 2304 | bytes 13824 | tf_op jit(solution)/shard_map/psum | solution.py:163
  656.9 48.4 %all-gather.8.cloned.1.call-done = bf16[1536,768]{1,0:T(8,128)(2,1)} async-done(((bf16[384,768]{1,0:T(8,128)(2,1)}), bf16[1536,768]{1,0:T(8,128)(2,1)}) %all-gather.8.cloned.1.call-update) | async-done | bytes 2359312 | tf_op jit(solution)/shard_map/all_gather | solution.py:194
  705.4 8.8 convert_reduce_fusion
  715.6 4.3 fusion.95
  720.7 83.4 %reduce-scatter.11.cloned.1.call-done = f32[384,768]{1,0:T(8,128)} async-done(((f32[1536,768]{1,0:T(8,128)}), f32[384,768]{1,0:T(8,128)}) %reduce-scatter.11.cloned.1.call-update) | async-done | bytes 1179664 | tf_op jit(solution)/shard_map/reduce_scatter | solution.py:205
  812.7 50.2 %all-gather.10.cloned.1.call-done = bf16[1536,768]{1,0:T(8,128)(2,1)} async-done(((bf16[384,768]{1,0:T(8,128)(2,1)}), bf16[1536,768]{1,0:T(8,128)(2,1)}) %all-gather.10.cloned.1.call-update) | async-done | bytes 2359312 | tf_op jit(solution)/shard_map/all_gather | solution.py:218
  867.4 74.8 %while.27 = (s32[]{:T(128)}, bf16[3,512,192]{1,2,0:T(8,128)(2,1)S(1)}, bf16[3,512,192]{1,2,0:T(8,128)(2,1)}, bf16[3,512,192]{1,2,0:T(8,128)(2,1)S(1)}, bf16[3,51...) while((s32[]{:T(128)}, ...), condition=%wide.region_20.21_spmd, body=%wide.region_18.20_spmd.sunk | while | flops 515084288 | bytes 27812488 | solution.py:225
  877.8 5.7 fusion.178
  886.6 5.6 fusion.176
  902.7 5.7 fusion.178
  911.6 5.6 fusion.176
  927.6 5.7 fusion.178
  936.5 5.6 fusion.176
  966.0 4.2 copy.87
  970.3 4.8 reshape.316
  975.3 4.6 bitcast_convert_fusion
  982.1 5.9 fusion.96
  988.1 6.7 fusion.58
  996.4 40.1 %all-reduce = (f32[768]{0:T(1024)}, f32[768]{0:T(1024)}, f32[768]{0:T(1024)}, f32[768]{0:T(1024)}, f32[768]{0:T(1024)}, /*index=5*/f32[768]{0:T(1024)}) all-reduce(f32[768]{0:T(1024)} %get-tuple-element.275, f32[768]{0:T(1024)} %get-tuple-element.222, ...), channel_id=1, replica_groups=mesh['dp'=8,'tensor'=4] {'dp','tensor'}, use_global_device_ids=true, to_apply=%region_28.29 | all-reduce | flops 4608 | bytes 36864 | tf_op jit(solution)/shard_map/psum | solution.py:269
  1036.8 25.2 %all-reduce.1 = (f32[2,192]{1,0:T(2,128)}, f32[768]{0:T(1024)}, f32[768]{0:T(1024)}, f32[768,3]{0,1:T(4,128)}, f32[3]{0:T(128)}) all-reduce(f32[2,192]{1,0:T(2,128)S(1)} %pad_maximum_fusion, f32[768]{0:T(1024)} %get-tuple-element.279, f32[768]{0:T(1024)} %get-tuple-element.301, ...), channel_id=1, replica_groups=mesh['dp'=8,'tensor'=4] {'dp'}, use_global_device_ids=true, to_apply=%region_25.26 | all-reduce | flops 4227 | bytes 33816 | tf_op jit(solution)/shard_map/psum | solution.py:280
  1065.5 21.0 %reduce-scatter.13.cloned.1.call-done = bf16[384,768]{1,0:T(8,128)(2,1)} async-done(((bf16[1536,768]{1,0:T(8,128)(2,1)}), bf16[384,768]{1,0:T(8,128)(2,1)}) %reduce-scatter.13.cloned.1.call-update) | async-done | bytes 589840 | tf_op jit(solution)/shard_map/reduce_scatter | solution.py:253
  1089.1 62.9 %all-reduce.7.cloned.1.call-done = f32[768,768]{1,0:T(8,128)} async-done(((f32[768,768]{1,0:T(8,128)}), f32[768,768]{1,0:T(8,128)}) %all-reduce.7.cloned.1.call-update) | async-done | bytes 2359312 | tf_op jit(solution)/shard_map/psum | solution.py:280
  1152.0 45.7 %reduce-scatter.17.cloned.1.call-done = f32[768,96]{0,1:T(8,128)} async-done(((f32[768,768]{0,1:T(8,128)}), f32[768,96]{0,1:T(8,128)}) %reduce-scatter.17.cloned.1.call-update) | async-done | bytes 294928 | tf_op jit(solution)/shard_map/reduce_scatter | solution.py:267
  1197.7 46.2 %reduce-scatter.15.cloned.1.call-done = f32[96,768]{1,0:T(8,128)} async-done(((f32[768,768]{1,0:T(8,128)}), f32[96,768]{1,0:T(8,128)}) %reduce-scatter.15.cloned.1.call-update) | async-done | bytes 294928 | tf_op jit(solution)/shard_map/reduce_scatter | solution.py:266
  (248 shorter events, 147.5 us)
Async XLA Ops:
  7.2 265.0 %copy-start = (bf16[768,768]{1,0:T(8,128)(2,1)S(1)}, bf16[768,768]{1,0:T(8,128)(2,1)}, u32[]{:S(2)}) copy-start(bf16[768,768]{1,0:T(8,128)(2,1)} %param.33) | copy-start | bytes 3538948
  7.2 55.1 %all-gather.6.cloned.1.call-start = ((), (), s32[]{:S(2)}) async-start(), calls=%async_computation.6 | async-start | bytes 2949120 | tf_op jit(solution)/shard_map/all_gather | solution.py:120
  7.9 257.5 %all-reduce.5.cloned.1.call-start = ((), (), s32[]{:S(2)}) async-start(), calls=%async_computation.7 | async-start | bytes 9437184 | tf_op jit(solution)/shard_map/psum | solution.py:137
  94.5 170.9 %copy-start.3 = (bf16[1536,768]{1,0:T(8,128)(2,1)S(1)}, bf16[1536,768]{1,0:T(8,128)(2,1)}, u32[]{:S(2)}) copy-start(bf16[1536,768]{1,0:T(8,128)(2,1)} %all-gather.6.cloned.1.call-done) | copy-start | bytes 7077892
  94.5 170.9 %copy-start.26 = (f32[768]{0:T(1024)S(1)}, f32[768]{0:T(1024)}, u32[]{:S(2)}) copy-start(f32[768]{0:T(1024)} %param.30) | copy-start | bytes 9220
  94.6 518.3 %all-gather.12.cloned.1.call-start = ((), (), s32[]{:S(2)}) async-start(), calls=%async_computation.15 | async-start | bytes 23592960 | tf_op jit(solution)/shard_map/all_gather | solution.py:149
  272.2 13.2 %copy-start.2 = (f32[1536,768]{1,0:T(8,128)}, f32[1536,768]{1,0:T(8,128)S(1)}, u32[]{:S(2)}) copy-start(f32[1536,768]{1,0:T(8,128)S(1)} %subtract_multiply_fusion.1) | copy-start | bytes 14155780
  272.2 14.7 %copy-start.39 = (bf16[768,768]{1,0:T(8,128)(2,1)S(1)}, bf16[768,768]{1,0:T(8,128)(2,1)}, u32[]{:S(2)}) copy-start(bf16[768,768]{1,0:T(8,128)(2,1)} %param.35) | copy-start | bytes 3538948
  291.1 414.2 %all-gather.8.cloned.1.call-start = ((), (), s32[]{:S(2)}) async-start(), calls=%async_computation.8 | async-start | bytes 2949120 | tf_op jit(solution)/shard_map/all_gather | solution.py:194
  612.8 10.4 copy-start.33
  628.6 19.9 %copy-start.16 = (bf16[768,768]{1,0:T(8,128)(2,1)S(1)}, bf16[768,768]{1,0:T(8,128)(2,1)}, u32[]{:S(2)}) copy-start(bf16[768,768]{1,0:T(8,128)(2,1)} %param.39) | copy-start | bytes 3538948
  628.6 19.9 %copy-start.34 = (f32[768]{0:T(1024)S(1)}, f32[768]{0:T(1024)}, u32[]{:S(2)}) copy-start(f32[768]{0:T(1024)} %param.40) | copy-start | bytes 9220
  628.6 20.1 %copy-start.40 = (bf16[768,3]{0,1:T(4,128)(2,1)S(1)}, bf16[768,3]{0,1:T(4,128)(2,1)}, u32[]{:S(2)}) copy-start(bf16[768,3]{0,1:T(4,128)(2,1)} %param.41) | copy-start | bytes 13828
  628.7 20.1 %copy-start.42 = (f32[3]{0:T(128)S(1)}, f32[3]{0:T(128)}, u32[]{:S(2)}) copy-start(f32[3]{0:T(128)} %param.42) | copy-start | bytes 40
  628.7 20.3 %copy-start.38 = (s32[3]{0:T(128)S(1)}, s32[3]{0:T(128)}, u32[]{:S(2)}) copy-start(s32[3]{0:T(128)} %param.26) | copy-start | bytes 40
  629.2 21.6 %copy-start.18 = (bf16[384,768]{1,0:T(8,128)(2,1)S(1)}, bf16[384,768]{1,0:T(8,128)(2,1)}, u32[]{:S(2)}) copy-start(bf16[384,768]{1,0:T(8,128)(2,1)} %param.43) | copy-start | bytes 1769476
  656.9 147.2 %reduce-scatter.11.cloned.1.call-start = ((), (), s32[]{:S(2)}) async-start(), calls=%async_computation.9 | async-start | bytes 5898240 | tf_op jit(solution)/shard_map/reduce_scatter | solution.py:205
  719.9 143.0 %all-gather.10.cloned.1.call-start = ((), (), s32[]{:S(2)}) async-start(), calls=%async_computation.10 | async-start | bytes 2949120 | tf_op jit(solution)/shard_map/all_gather | solution.py:218
  720.7 87.5 %copy-start.29 = (f32[384]{0:T(512)}, f32[384]{0:T(512)S(1)}, u32[]{:S(2)}) copy-start(f32[384]{0:T(512)S(1)} %dynamic-slice.6) | copy-start | bytes 4612
  808.2 54.7 %copy-start.19 = (bf16[192,768]{1,0:T(8,128)(2,1)S(1)}, bf16[192,768]{1,0:T(8,128)(2,1)}, u32[]{:S(2)}) copy-start(bf16[192,768]{1,0:T(8,128)(2,1)} %param.29) | copy-start | bytes 884740
  808.2 57.3 %copy-start.30 = (f32[384]{0:T(512)}, f32[384]{0:T(512)S(1)}, u32[]{:S(2)}) copy-start(f32[384]{0:T(512)S(1)} %broadcast_multiply_fusion.2) | copy-start | bytes 4612
  808.2 57.3 %copy-start.31 = (f32[384]{0:T(512)}, f32[384]{0:T(512)S(1)}, u32[]{:S(2)}) copy-start(f32[384]{0:T(512)S(1)} %broadcast_multiply_fusion.3) | copy-start | bytes 4612
  812.3 249.7 %reduce-scatter.21.cloned.1.call-start = ((), (), s32[]{:S(2)}) async-start(), calls=%async_computation.17 | async-start | bytes 884736
  942.2 9.8 copy-start.11
  957.9 105.7 %reduce-scatter.19.cloned.1.call-start = ((), (), s32[]{:S(2)}) async-start(), calls=%async_computation.16 | async-start | bytes 2211840
  975.1 111.4 %reduce-scatter.13.cloned.1.call-start = ((), (), s32[]{:S(2)}) async-start(), calls=%async_computation.11 | async-start | bytes 2949120 | tf_op jit(solution)/shard_map/reduce_scatter | solution.py:253
  980.0 172.0 %all-reduce.7.cloned.1.call-start = ((), (), s32[]{:S(2)}) async-start(), calls=%async_computation.14 | async-start | bytes 4718592 | tf_op jit(solution)/shard_map/psum | solution.py:280
  982.1 215.6 %reduce-scatter.17.cloned.1.call-start = ((), (), s32[]{:S(2)}) async-start(), calls=%async_computation.13 | async-start | bytes 2654208 | tf_op jit(solution)/shard_map/reduce_scatter | solution.py:267
  988.0 48.5 %copy-start.12 = (bf16[3,512,192]{1,2,0:T(8,128)(2,1)S(1)}, bf16[3,512,192]{1,2,0:T(8,128)(2,1)}, u32[]{:S(2)}) copy-start(bf16[3,512,192]{1,2,0:T(8,128)(2,1)} %copy-done.11) | copy-start | bytes 1769476
  988.0 255.8 %reduce-scatter.15.cloned.1.call-start = ((), (), s32[]{:S(2)}) async-start(), calls=%async_computation.12 | async-start | bytes 2654208 | tf_op jit(solution)/shard_map/reduce_scatter | solution.py:266
  994.8 41.8 %copy-start.14 = (bf16[3,512,192]{1,2,0:T(8,128)(2,1)S(1)}, bf16[3,512,192]{1,2,0:T(8,128)(2,1)}, u32[]{:S(2)}) copy-start(bf16[3,512,192]{1,2,0:T(8,128)(2,1)} %copy-done.13) | copy-start | bytes 1769476
  994.8 91.7 %copy-start.10 = (f32[384,768]{1,0:T(8,128)S(1)}, f32[384,768]{1,0:T(8,128)}, u32[]{:S(2)}) copy-start(f32[384,768]{1,0:T(8,128)} %copy-done.9) | copy-start | bytes 3538948
  (25 other events, 79.0 us)
Sparse Core Ops, SparseCore 0:
  9.6 52.6 all-gather.5
  94.7 170.7 all-reduce.4
  291.3 321.5 all-gather.11
  657.0 48.3 all-gather.7
  720.0 84.0 reduce-scatter.10
  812.4 50.4 all-gather.9
  958.0 33.6 reduce-scatter.20
  995.2 40.5 reduce-scatter.18
  1038.7 47.7 reduce-scatter.12
  1089.6 62.3 all-reduce.6
  1155.9 41.6 reduce-scatter.16
  1201.4 42.3 reduce-scatter.14
